TPU v7x, 8 devices: a whole 2x2x1 slice. The times are simulated.
8 devices in a mesh: dp: 1 (over z), cp: 8 (over y, x, core).
Axes of the slice: x: 2, y: 2, z: 1, core: 2. Of those that a mesh axis runs over, the one named last changes fastest.
Arguments:
- x_in: bfloat16 [1024, 3072], P(('dp', 'cp'))
- d_y: bfloat16 [1024, 3072], P(('dp', 'cp'))
- w_q: bfloat16 [3072, 24, 128], replicated
- w_k: bfloat16 [3072, 8, 128], replicated
- w_v: bfloat16 [3072, 8, 128], replicated
- w_o: bfloat16 [24, 128, 3072], replicated
Outputs:
- output: bfloat16 [1024, 3072], P(('dp', 'cp'))
All inputs are finite; a program needn't handle non-finite values.
Results may differ from a plain program's by a relative error of at most 0.0114857.
Values are sent between devices in bfloat16 or wider.
A program may use at most 1 GiB of HBM per device.

v0:
```python
import math

import jax
import jax.numpy as jnp
from jax import lax
from jax.experimental import pallas as pl
from jax.experimental.pallas import tpu as pltpu
from jax.sharding import PartitionSpec as P

MESH = pl.DeviceIdType.MESH
BF16, F32 = jnp.bfloat16, jnp.float32
NT = (((1,), (1,)), ((), ()))

N_DEV, N_CHIP, TOK, SEG = 8, 4, 128, 64
ROWS = 2 * TOK
SEQ = N_DEV * TOK
D = 3072
HD = 128
G = 3
BQ = 256
NB = SEQ // BQ
C = HD**-0.5
C2 = C * math.log2(math.e)
U_DO, U_K, U_V, U_Q = 0, 3, 4, 5
SLOTS = 12
RB = 128
ND = 3072
NV = 3072
VLIM = 66_000_000

scope = jax.named_scope


def dot_nt(a, b):
    return lax.dot_general(a, b, NT, preferred_element_type=F32)


def dot(a, b):
    return jnp.dot(a, b, preferred_element_type=F32)


def kernel(x_hbm, dy_hbm, wq_hbm, wk_hbm, wv_hbm, wo_hbm, out_ref,
           x_v, dy_v, wo_s, w_s, wq_r, wk_r, wv_r, sbuf, recv, obuf, rin, rkv, acc, pbuf,
           s0, s1, s2, s3, d0, d1, d2, d3, p0, p1, p2, p3, e0, e1, e2, e3, kt, vt, dk_acc, dv_acc,
           io_sem, wo_sem, w_sem, xs_sem, xr_sem, send_sem, recv_sem, osend_sem, orecv_sem, kv_sem, ps_sem, pr_sem):
    s_scr, dp_scr, p_scr, ds_scr = (s0, s1, s2, s3), (d0, d1, d2, d3), (p0, p1, p2, p3), (e0, e1, e2, e3)
    me = lax.axis_index("cp")
    dp = lax.axis_index("dp")
    chip = me // 2
    q = lax.rem(me, 2)
    partner = (dp, 2 * chip + 1 - q)

    def peer(k):
        return lax.rem(chip + k, N_CHIP)

    def dev_of(cc):
        return (dp, 2 * cc + q)

    barrier = pltpu.get_barrier_semaphore()
    pl.semaphore_signal(barrier, inc=1, device_id=partner, device_id_type=MESH)
    for k in range(1, N_CHIP):
        pl.semaphore_signal(barrier, inc=1, device_id=dev_of(peer(k)), device_id_type=MESH)

    def tok_rows(i):
        return pl.ds(pl.multiple_of(i * TOK, TOK), TOK)

    def chip_rows(i):
        return pl.ds(pl.multiple_of(i * ROWS, ROWS), ROWS)

    own, other = tok_rows(q), tok_rows(1 - q)

    def io_copy(n):
        src, dst = ((dy_hbm, dy_v), (x_hbm, x_v))[n]
        return pltpu.make_async_copy(src, dst.at[own], io_sem.at[n])

    def swap_copy(n):
        ref = (dy_v, x_v)[n]
        return pltpu.make_async_remote_copy(
            src_ref=ref.at[own], dst_ref=ref.at[own], send_sem=xs_sem.at[n], recv_sem=xr_sem.at[n],
            device_id=partner, device_id_type=MESH)

    def wo_copy(g, k):
        return pltpu.make_async_copy(wo_hbm.at[q, peer(k), g], wo_s.at[g % 2, k - 1], wo_sem.at[g % 2, k - 1])

    def wkv_copy(w_hbm, i, slot, half=None):
        half = q if half is None else half
        return pltpu.make_async_copy(w_hbm.at[i, :, :, half], w_s.at[slot], w_sem.at[slot])

    def wq_copy(i, slot):
        return pltpu.make_async_copy(wq_hbm.at[i, :, pl.ds(3 * q, 3)], w_s.at[slot], w_sem.at[slot])

    def wait_slot(slot):
        wkv_copy(wk_hbm, 0, slot).wait()

    io_copy(0).start()
    for k in (1, 2):
        wo_copy(0, k).start()
    dk_acc[...] = jnp.zeros_like(dk_acc)
    dv_acc[...] = jnp.zeros_like(dv_acc)
    with scope('barrier'):
        pl.semaphore_wait(barrier, N_CHIP)
    io_copy(1).start()
    for i in range(4):
        wkv_copy(wk_hbm, i, i).start()
    with scope('swapdy'):
        io_copy(0).wait()
        swap_copy(0).start()

    def relay_kv(dst, base, i, slot):
        flat = w_s.at[slot].reshape(768 * 4, HD)
        for h in range(4):
            for r in range(0, 768, RB):
                dst[base + h, pl.ds(i * 768 + r, RB), :] = flat[pl.ds(4 * r + h, RB, stride=4), :]

    def relay_q(i, slot):
        flat = w_s.at[slot].reshape(768 * 4, HD)
        for h in range(12):
            for r in range(0, 256, RB):
                wq_r[h, pl.ds(i * 256 + r, RB), :] = flat[pl.ds(12 * r + h, RB, stride=12), :]


    def send_part(unit, k, val, rows, dst_rows):
        if k == N_CHIP:
            recv[unit, dst_rows, :] = val
            return
        sbuf[unit, k - 1, rows, :] = val
        pltpu.make_async_remote_copy(
            src_ref=sbuf.at[unit, k - 1, rows], dst_ref=recv.at[unit, dst_rows],
            send_sem=send_sem, recv_sem=recv_sem.at[unit],
            device_id=dev_of(peer(k)), device_id_type=MESH).start()

    def send_rows(unit, k, val, r):
        send_part(unit, k, val, tok_rows(r), tok_rows(2 * chip + r))

    def send_block(unit, k, val):
        send_part(unit, k, val, pl.ds(0, ROWS), chip_rows(chip))

    def do0_rows(r, ks):
        w = wo_s[0, pl.ds(ks[0] - 1, len(ks))].reshape(len(ks) * HD, D)
        val = dot_nt(dy_v[tok_rows(r), :], w).astype(BF16)
        for n, k in enumerate(ks):
            send_rows(U_DO, k, val[:, n * HD:(n + 1) * HD], r)

    def do_steps(g):
        for k in range(1, 5):
            wo_copy(g, k).wait()
        val = dot_nt(dy_v[...], wo_s[g % 2].reshape(4 * HD, D)).astype(BF16)
        for k in range(1, 5):
            send_block(U_DO + g, k, val[:, (k - 1) * HD:k * HD])

    def k_rows(r):
        w = jnp.concatenate([wk_r[4 * q + peer(k)] for k in range(1, 5)], axis=1)
        val = dot(x_v[tok_rows(r), :], w).astype(BF16)
        for k in range(1, 5):
            send_rows(U_K, k, val[:, (k - 1) * HD:k * HD], r)

    def v_steps():
        w = jnp.concatenate([wv_r[4 * q + peer(k)] for k in range(1, 5)], axis=1)
        val = dot(x_v[...], w).astype(BF16)
        for k in range(1, 5):
            send_block(U_V, k, val[:, (k - 1) * HD:k * HD])

    def q_steps(g):
        w = jnp.concatenate([wq_r[3 * peer(k) + g] for k in range(1, 5)], axis=1)
        val = dot(x_v[...], w).astype(BF16)
        for k in range(1, 5):
            send_block(U_Q + g, k, val[:, (k - 1) * HD:k * HD])

    with scope('do0a'):
        for k in (1, 2):
            wo_copy(0, k).wait()
        do0_rows(q, (1, 2))
    for i in range(4):
        wkv_copy(wv_hbm, i, 4 + i).start()
    with scope('swapx'):
        io_copy(1).wait()
        swap_copy(1).start()
    with scope('relk'):
        for i in range(4):
            wait_slot(i)
            relay_kv(wk_r, 4 * q, i, i)
    for k in (3, 4):
        wo_copy(0, k).start()
    with scope('k_own'):
        k_rows(q)
    with scope('xswap'):
        swap_copy(1).wait_recv()
    with scope('k_other'):
        k_rows(1 - q)
    with scope('relv'):
        for i in range(4):
            wait_slot(4 + i)
            relay_kv(wv_r, 4 * q, i, 4 + i)
    for i in range(4):
        wq_copy(i, 8 + i).start()
    with scope('v'):
        v_steps()
    for i in range(4):
        wq_copy(4 + i, i).start()
    with scope('do0b'):
        for k in (3, 4):
            wo_copy(0, k).wait()
        do0_rows(q, (3, 4))
    for i in range(4):
        wq_copy(8 + i, 4 + i).start()
    with scope('dyswap'):
        swap_copy(0).wait_recv()
    with scope('do0c'):
        do0_rows(1 - q, (1, 2, 3, 4))
    for k in range(1, 5):
        wo_copy(1, k).start()
    with scope('relq'):
        for i in range(12):
            slot = (8 + i) % SLOTS
            wait_slot(slot)
            relay_q(i, slot)
    for k in range(1, 5):
        wo_copy(2, k).start()
    with scope('q0'):
        q_steps(0)
    for i in range(8):
        wkv_copy((wk_hbm, wv_hbm)[i // 4], i % 4, (8 + i) % SLOTS, 1 - q).start()
    for g in (1, 2):
        with scope('do12'):
            do_steps(g)
        with scope('q12'):
            q_steps(g)
    with scope('relkv2'):
        for i in range(4):
            wait_slot(8 + i)
            relay_kv(wk_r, 4 - 4 * q, i, 8 + i)
            wait_slot(i)
            relay_kv(wv_r, 4 - 4 * q, i, i)

    def wait_unit(u):
        part = recv.at[u, pl.ds(0, SEQ - ROWS)]
        pltpu.make_async_copy(part, part, recv_sem.at[u]).wait()

    with scope('waitkv'):
        wait_unit(U_K)
        wait_unit(U_V)
    def segs(b):
        out = []
        for seg in range(4 * b, 4 * b + 4):
            row = seg * TOK if seg < N_DEV else (2 * N_DEV - 1 - seg) * TOK + SEG
            out.append(slice(row, row + SEG))
        return out

    def pos_block(u, b):
        return jnp.concatenate([recv[u, r, :] for r in segs(b)], axis=0)

    def put_block(u, b, val):
        for n, r in enumerate(segs(b)):
            obuf[u, r, :] = val[n * SEG:(n + 1) * SEG]

    for b in range(NB):
        kt[:, b * BQ:(b + 1) * BQ] = pos_block(U_K, b).T
        vt[:, b * BQ:(b + 1) * BQ] = pos_block(U_V, b).T

    def send_out(u):
        slot = G * chip + u
        for k in range(1, N_CHIP):
            pltpu.make_async_remote_copy(
                src_ref=obuf.at[u, chip_rows(peer(k))], dst_ref=rin.at[slot],
                send_sem=osend_sem, recv_sem=orecv_sem.at[u],
                device_id=dev_of(peer(k)), device_id_type=MESH).start()
        rin[slot] = obuf[u, chip_rows(chip), :]

    def attn_head(g, _):
        with scope('waitq'):
            wait_unit(U_DO + g)
            wait_unit(U_Q + g)
        st = [{} for _ in range(NB)]

        def chunks(b):
            return [slice(k * BQ, (k + 1) * BQ) for k in range(b + 1)]

        def scores(b):
            qb = pos_block(U_Q + g, b)
            dob = pos_block(U_DO + g, b)
            mx = None
            for kc, ks in enumerate(chunks(b)):
                s = dot_nt(pos_block(U_K, kc), qb)
                if kc == b:
                    key = lax.broadcasted_iota(jnp.int32, (BQ, BQ), 0)
                    qry = lax.broadcasted_iota(jnp.int32, (BQ, BQ), 1)
                    s = jnp.where(key <= qry, s, -jnp.inf)
                s_scr[b][ks, :] = s
                mc = jnp.max(s.reshape(BQ // 8, 8, BQ), axis=0)
                mx = mc if mx is None else jnp.maximum(mx, mc)
            for kc, ks in enumerate(chunks(b)):
                dp_scr[b][ks, :] = dot_nt(pos_block(U_V, kc), dob)
            st[b]['m2'] = jnp.max(mx, axis=0, keepdims=True) * C2

        def probs(b):
            m2 = st[b]['m2']
            ls = None
            for ks in chunks(b):
                e = jnp.exp2(s_scr[b][ks, :] * C2 - m2)
                lc = jnp.sum(e.reshape(BQ // 8, 8, BQ), axis=0)
                ls = lc if ls is None else ls + lc
            lse2 = m2 + jnp.log2(jnp.sum(ls, axis=0, keepdims=True))
            for ks in chunks(b):
                p_scr[b][ks, :] = jnp.exp2(s_scr[b][ks, :] * C2 - lse2).astype(BF16)

        def outs(b):
            n = (b + 1) * BQ
            dob = pos_block(U_DO + g, b)
            ot = dot(vt[:, :n], p_scr[b][...]).astype(BF16)
            st[b]['delta'] = jnp.sum(dob.T.astype(F32) * ot.astype(F32), axis=0, keepdims=True)
            for ks in chunks(b):
                dv_acc[ks, :] += dot(p_scr[b][ks, :], dob)

        def dscores(b):
            delta = st[b]['delta']
            for ks in chunks(b):
                ds_scr[b][ks, :] = (p_scr[b][ks, :].astype(F32) * (dp_scr[b][ks, :] - delta)).astype(BF16)

        def grads(b):
            n = (b + 1) * BQ
            qb = pos_block(U_Q + g, b)
            for ks in chunks(b):
                dk_acc[ks, :] += dot(ds_scr[b][ks, :], qb)
            dqt = (dot(kt[:, :n], ds_scr[b][...]) * C).astype(BF16)
            put_block(g, b, dqt.T)

        with scope('attn'):
            scores(3)
            scores(2)
            probs(3)
            outs(3)
            scores(1)
            dscores(3)
            probs(2)
            grads(3)
            outs(2)
            scores(0)
            dscores(2)
            probs(1)
            grads(2)
            outs(1)
            dscores(1)
            probs(0)
            grads(1)
            outs(0)
            dscores(0)
            grads(0)

        with scope('send'):
            send_out(g)
        return 0

    lax.fori_loop(0, G, attn_head, 0)
    def send_owners(n):
        slot = 8 * n + 4 * q + chip

        def send_dev(dev, part):
            pltpu.make_async_remote_copy(
                src_ref=obuf.at[G + n, tok_rows(dev)], dst_ref=rkv.at[slot],
                send_sem=osend_sem, recv_sem=kv_sem.at[n, part],
                device_id=(dp, dev), device_id_type=MESH).start()

        send_dev(partner[1], 0)
        for k in range(1, N_CHIP):
            for r in range(2):
                send_dev(2 * peer(k) + r, k if n == 1 else 1)
        rkv[slot] = obuf[G + n, tok_rows(me), :]

    with scope('senddkv'):
        for b in range(NB):
            put_block(3, b, (dk_acc[b * BQ:(b + 1) * BQ, :] * C).astype(BF16))
        send_owners(0)
        for b in range(NB):
            put_block(4, b, dv_acc[b * BQ:(b + 1) * BQ, :].astype(BF16))
        send_owners(1)

    def p_copy():
        return pltpu.make_async_remote_copy(
            src_ref=acc.at[other], dst_ref=pbuf, send_sem=ps_sem, recv_sem=pr_sem,
            device_id=partner, device_id_type=MESH)

    def wait_kv(n, part, count):
        ref = obuf.at[0, pl.ds(0, count * TOK)]
        pltpu.make_async_copy(ref, ref, kv_sem.at[n, part]).wait()

    def kv_dx(items, last=False):
        lhs, rhs = [], []
        for n, k in items:
            c = lax.rem(chip + N_CHIP - k, N_CHIP)
            for r in range(2):
                lhs.append(rkv[8 * n + 4 * r + c])
                rhs.append((wk_r, wv_r)[n][4 * r + c])
        t = dot_nt(jnp.concatenate(lhs, axis=1), jnp.concatenate(rhs, axis=1)) + acc[own, :]
        if last:
            out_ref[...] = (t + pbuf[...]).astype(BF16)
        else:
            acc[own, :] = t

    for u in range(G):
        with scope('waito'):
            part = obuf.at[u, pl.ds(0, SEQ - ROWS)]
            pltpu.make_async_copy(part, part, orecv_sem.at[u]).wait()
        with scope('dx'):
            t = dot_nt(jnp.concatenate([rin[G * j + u] for j in range(N_CHIP)], axis=1),
                       jnp.concatenate([wq_r[G * j + u] for j in range(N_CHIP)], axis=1))
            acc[...] = t if u == 0 else t + acc[...]
        if u == 0:
            with scope('kvlocal'):
                wait_kv(0, 0, 1)
                wait_kv(1, 0, 1)
                kv_dx([(0, 0), (1, 0)])
    p_copy().start()

    with scope('waitk'):
        wait_kv(0, 1, 6)
    with scope('kdx'):
        kv_dx([(0, 1), (0, 2), (0, 3)])
    for k in (1, 2):
        with scope('waitv%d' % k):
            wait_kv(1, k, 2)
        with scope('vdx%d' % k):
            kv_dx([(1, k)])
    with scope('waitv3'):
        wait_kv(1, 3, 2)
    with scope('waitp'):
        p_copy().wait_recv()
    with scope('vdx3'):
        kv_dx([(1, 3)], last=True)

    with scope('final'):
        for n in range(2):
            swap_copy(n).wait_send()
        p_copy().wait_send()
        pltpu.make_async_copy(sbuf, sbuf, send_sem).wait()
        part = obuf.at[pl.ds(0, G), pl.ds(0, SEQ - ROWS)]
        pltpu.make_async_copy(part, part, osend_sem).wait()
        part = obuf.at[pl.ds(0, 2), pl.ds(0, SEQ - TOK)]
        pltpu.make_async_copy(part, part, osend_sem).wait()


def write_out(src, dst, sem):
    cp = pltpu.make_async_copy(src, dst, sem)
    cp.start()
    cp.wait()


def solution(mesh):
    row_spec = P(("dp", "cp"), None)

    def device_fn(x_in, d_y, w_q, w_k, w_v, w_o):
        dma = pltpu.SemaphoreType.DMA
        res = pl.pallas_call(
            kernel,
            out_shape=pltpu.VMEM((TOK, D), BF16),
            in_specs=[pl.BlockSpec(memory_space=pl.ANY)] * 6,
            out_specs=pl.BlockSpec(memory_space=pltpu.VMEM),
            scratch_shapes=[
                pltpu.VMEM((ROWS, D), BF16),
                pltpu.VMEM((ROWS, D), BF16),
                pltpu.VMEM((2, N_CHIP, HD, D), BF16),
                pltpu.VMEM((SLOTS, 256, 3, 4, HD), BF16),
                pltpu.VMEM((12, D, HD), BF16),
                pltpu.VMEM((8, D, HD), BF16),
                pltpu.VMEM((8, D, HD), BF16),
                pltpu.VMEM((8, 3, ROWS, HD), BF16),
                pltpu.VMEM((8, SEQ, HD), BF16),
                pltpu.VMEM((5, SEQ, HD), BF16),
                pltpu.VMEM((12, ROWS, HD), BF16),
                pltpu.VMEM((16, TOK, HD), BF16),
                pltpu.VMEM((ROWS, D), F32),
                pltpu.VMEM((TOK, D), F32),
                *[pltpu.VMEM(((b + 1) * BQ, BQ), t) for t in (F32, F32, BF16, BF16) for b in range(NB)],
                pltpu.VMEM((HD, SEQ), BF16),
                pltpu.VMEM((HD, SEQ), BF16),
                pltpu.VMEM((SEQ, HD), F32),
                pltpu.VMEM((SEQ, HD), F32),
                dma((2,)), dma((2, N_CHIP)), dma((SLOTS,)), dma((2,)), dma((2,)),
                dma, dma((8,)), dma, dma((G,)), dma((2, 4)), dma, dma,
            ],
            compiler_params=pltpu.CompilerParams(
                collective_id=0, has_side_effects=True, vmem_limit_bytes=VLIM),
        )(x_in, d_y, w_q.reshape(12, 256, 6, 4, HD), w_k.reshape(4, 256, 3, 2, 4, HD), w_v.reshape(4, 256, 3, 2, 4, HD),
          w_o.reshape(2, N_CHIP, G, HD, D))
        return pl.pallas_call(
            write_out,
            out_shape=jax.ShapeDtypeStruct((TOK, D), BF16),
            in_specs=[pl.BlockSpec(memory_space=pltpu.VMEM)],
            out_specs=pl.BlockSpec(memory_space=pl.ANY),
            scratch_shapes=[pltpu.SemaphoreType.DMA],
        )(pltpu.with_memory_space_constraint(res, pltpu.VMEM))

    return jax.shard_map(device_fn, mesh=mesh, in_specs=(row_spec, row_spec, P(), P(), P(), P()),
                         out_specs=row_spec, check_vma=False)
```

profile of v0, /device:TPU:0, one launch (start us, length us, event | category | flops | bytes accessed | tf_op | source)
XLA Modules:
  0.0 47.5 jit_solution(12468646443138459874)
XLA Ops:
  0.0 46.4 %shard_map.64.src = bf16[128,3072]{1,0:T(8,128)(2,1)S(1)} custom-call(bf16[128,3072]{1,0:T(8,128)(2,1)} %x_hbm.1, bf16[128,3072]{1,0:T(8,128)(2,1)} %dy_hbm.1, bf16[12,256,6,4,128]{4,3,2,1,0:T(4,128)(2,1)} %bitcast.4, bf16[4,256,3,2,4,128]{5,4,3,2,1,0:T(4,128)(2,1)} %bitcast.6, bf16[4,256,3,2,4,128]{5,4,3,2,1,0:T(4,128)(2,1)} %bitcast.7, ...), custom_call_target="tpu_custom_call" | custom-call | tf_op jit(solution)/shard_map/pallas_call | solution.py:452
  46.4 0.9 %shard_map.65 = bf16[128,3072]{1,0:T(8,128)(2,1)} custom-call(bf16[128,3072]{1,0:T(8,128)(2,1)S(1)} %shard_map.64.src), custom_call_target="tpu_custom_call" | custom-call | tf_op jit(solution)/shard_map/pallas_call | solution.py:484
where the time goes:
time: 47.6 us; the launch traced here: 47.5 us
  Pallas kernels  47.3 us (99%)
    pallas_call x1, Pallas kernels, device_fn(): pl.pallas_call(kernel, out_shape=pltpu.VMEM((TOK, D), BF16), in_specs=[pl...  46.4 us

commit v1 on v0

--- a/solution.py
+++ b/solution.py
@@ -93,18 +93,19 @@
         wkv_copy(wk_hbm, 0, slot).wait()
 
     io_copy(0).start()
+    io_copy(1).start()
     for k in (1, 2):
         wo_copy(0, k).start()
     dk_acc[...] = jnp.zeros_like(dk_acc)
     dv_acc[...] = jnp.zeros_like(dv_acc)
     with scope('barrier'):
         pl.semaphore_wait(barrier, N_CHIP)
-    io_copy(1).start()
     for i in range(4):
         wkv_copy(wk_hbm, i, i).start()
-    with scope('swapdy'):
+    with scope('swapx'):
+        io_copy(1).wait()
+        swap_copy(1).start()
         io_copy(0).wait()
-        swap_copy(0).start()
 
     def relay_kv(dst, base, i, slot):
         flat = w_s.at[slot].reshape(768 * 4, HD)
@@ -172,9 +173,7 @@
         do0_rows(q, (1, 2))
     for i in range(4):
         wkv_copy(wv_hbm, i, 4 + i).start()
-    with scope('swapx'):
-        io_copy(1).wait()
-        swap_copy(1).start()
+    swap_copy(0).start()
     with scope('relk'):
         for i in range(4):
             wait_slot(i)
@@ -438,12 +437,6 @@
         pltpu.make_async_copy(part, part, osend_sem).wait()
 
 
-def write_out(src, dst, sem):
-    cp = pltpu.make_async_copy(src, dst, sem)
-    cp.start()
-    cp.wait()
-
-
 def solution(mesh):
     row_spec = P(("dp", "cp"), None)
 
@@ -481,13 +474,7 @@
                 collective_id=0, has_side_effects=True, vmem_limit_bytes=VLIM),
         )(x_in, d_y, w_q.reshape(12, 256, 6, 4, HD), w_k.reshape(4, 256, 3, 2, 4, HD), w_v.reshape(4, 256, 3, 2, 4, HD),
           w_o.reshape(2, N_CHIP, G, HD, D))
-        return pl.pallas_call(
-            write_out,
-            out_shape=jax.ShapeDtypeStruct((TOK, D), BF16),
-            in_specs=[pl.BlockSpec(memory_space=pltpu.VMEM)],
-            out_specs=pl.BlockSpec(memory_space=pl.ANY),
-            scratch_shapes=[pltpu.SemaphoreType.DMA],
-        )(pltpu.with_memory_space_constraint(res, pltpu.VMEM))
+        return res
 
     return jax.shard_map(device_fn, mesh=mesh, in_specs=(row_spec, row_spec, P(), P(), P(), P()),
                          out_specs=row_spec, check_vma=False)

time: 47.6 us -> 46.8 us (0.983)
  Pallas kernels: 47.3 us -> 45.8 us
  local copies, waits for them, and re-layouts: 0 us -> 0.88 us
    pallas_call x1 -> x0, Pallas kernels: 0.89 us -> none  [device_fn(): pl.pallas_call(write_out, out_shape=jax.ShapeDtypeStruct((TOK, D), BF16),...]
    unnamed x0 -> x1, local copies, waits for them, and re-layouts: none -> 0.88 us
    pallas_call x1, Pallas kernels: 46.4 us -> 45.8 us  [device_fn(): pl.pallas_call(kernel, out_shape=pltpu.VMEM((TOK, D), BF16), in_specs=[pl...]
where the time goes in v1:
time: 46.8 us; the launch traced here: 46.7 us
  Pallas kernels  45.8 us (98%)
  local copies, waits for them, and re-layouts  0.88 us (2%)
    pallas_call x1, Pallas kernels, device_fn(): pl.pallas_call(kernel, out_shape=pltpu.VMEM((TOK, D), BF16), in_specs=[pl...  45.8 us

profile of v1, /device:TPU:0, one launch (start us, length us, event | category | flops | bytes accessed | tf_op | source)
XLA Modules:
  0.0 46.7 jit_solution(8402490314314739482)
XLA Ops:
  0.0 45.8 %shard_map.64 = bf16[128,3072]{1,0:T(8,128)(2,1)S(1)} custom-call(bf16[128,3072]{1,0:T(8,128)(2,1)} %x_hbm.1, bf16[128,3072]{1,0:T(8,128)(2,1)} %dy_hbm.1, bf16[12,256,6,4,128]{4,3,2,1,0:T(4,128)(2,1)} %bitcast.4, bf16[4,256,3,2,4,128]{5,4,3,2,1,0:T(4,128)(2,1)} %bitcast.6, bf16[4,256,3,2,4,128]{5,4,3,2,1,0:T(4,128)(2,1)} %bitcast.7, ...), custom_call_target="tpu_custom_call" | custom-call | tf_op jit(solution)/shard_map/pallas_call | solution.py:445
  45.8 0.9 %copy.8 = bf16[128,3072]{1,0:T(8,128)(2,1)} copy(bf16[128,3072]{1,0:T(8,128)(2,1)S(1)} %shard_map.64) | data formatting | bytes 1572864

commit v2 on v1

--- a/solution.py
+++ b/solution.py
@@ -100,6 +100,7 @@
     dv_acc[...] = jnp.zeros_like(dv_acc)
     with scope('barrier'):
         pl.semaphore_wait(barrier, N_CHIP)
+    wo_copy(0, 3).start()
     for i in range(4):
         wkv_copy(wk_hbm, i, i).start()
     with scope('swapx'):
@@ -171,15 +172,17 @@
         for k in (1, 2):
             wo_copy(0, k).wait()
         do0_rows(q, (1, 2))
+    swap_copy(0).start()
     for i in range(4):
         wkv_copy(wv_hbm, i, 4 + i).start()
-    swap_copy(0).start()
+    with scope('do0a3'):
+        wo_copy(0, 3).wait()
+        do0_rows(q, (3,))
     with scope('relk'):
         for i in range(4):
             wait_slot(i)
             relay_kv(wk_r, 4 * q, i, i)
-    for k in (3, 4):
-        wo_copy(0, k).start()
+    wo_copy(0, 4).start()
     with scope('k_own'):
         k_rows(q)
     with scope('xswap'):
@@ -197,9 +200,8 @@
     for i in range(4):
         wq_copy(4 + i, i).start()
     with scope('do0b'):
-        for k in (3, 4):
-            wo_copy(0, k).wait()
-        do0_rows(q, (3, 4))
+        wo_copy(0, 4).wait()
+        do0_rows(q, (4,))
     for i in range(4):
         wq_copy(8 + i, 4 + i).start()
     with scope('dyswap'):

time: 46.8 us -> 47 us (level)
  no operation moved by 1% of the time
where the time goes in v2:
time: 47 us; the launch traced here: 46.9 us
  Pallas kernels  46 us (98%)
  local copies, waits for them, and re-layouts  0.88 us (2%)
    pallas_call x1, Pallas kernels, device_fn(): pl.pallas_call(kernel, out_shape=pltpu.VMEM((TOK, D), BF16), in_specs=[pl...  46 us

profile of v2, /device:TPU:0, one launch (start us, length us, event | category | flops | bytes accessed | tf_op | source)
XLA Modules:
  0.0 46.9 jit_solution(15350586109911443779)
XLA Ops:
  0.0 46.0 %shard_map.64 = bf16[128,3072]{1,0:T(8,128)(2,1)S(1)} custom-call(bf16[128,3072]{1,0:T(8,128)(2,1)} %x_hbm.1, bf16[128,3072]{1,0:T(8,128)(2,1)} %dy_hbm.1, bf16[12,256,6,4,128]{4,3,2,1,0:T(4,128)(2,1)} %bitcast.4, bf16[4,256,3,2,4,128]{5,4,3,2,1,0:T(4,128)(2,1)} %bitcast.6, bf16[4,256,3,2,4,128]{5,4,3,2,1,0:T(4,128)(2,1)} %bitcast.7, ...), custom_call_target="tpu_custom_call" | custom-call | tf_op jit(solution)/shard_map/pallas_call | solution.py:447
  46.0 0.9 %copy.8 = bf16[128,3072]{1,0:T(8,128)(2,1)} copy(bf16[128,3072]{1,0:T(8,128)(2,1)S(1)} %shard_map.64) | data formatting | bytes 1572864

commit v3 on v1

--- a/solution.py
+++ b/solution.py
@@ -171,17 +171,17 @@
         for k in (1, 2):
             wo_copy(0, k).wait()
         do0_rows(q, (1, 2))
-    for i in range(4):
-        wkv_copy(wv_hbm, i, 4 + i).start()
-    swap_copy(0).start()
     with scope('relk'):
         for i in range(4):
             wait_slot(i)
             relay_kv(wk_r, 4 * q, i, i)
+    for i in range(4):
+        wkv_copy(wv_hbm, i, 4 + i).start()
+    with scope('k_own'):
+        k_rows(q)
     for k in (3, 4):
         wo_copy(0, k).start()
-    with scope('k_own'):
-        k_rows(q)
+    swap_copy(0).start()
     with scope('xswap'):
         swap_copy(1).wait_recv()
     with scope('k_other'):

time: 46.8 us -> 46.8 us (level)
  no operation moved by 1% of the time
where the time goes in v3:
time: 46.8 us; the launch traced here: 46.7 us
  Pallas kernels  45.8 us (98%)
  local copies, waits for them, and re-layouts  0.88 us (2%)
    pallas_call x1, Pallas kernels, device_fn(): pl.pallas_call(kernel, out_shape=pltpu.VMEM((TOK, D), BF16), in_specs=[pl...  45.8 us

profile of v3, /device:TPU:0, one launch (start us, length us, event | category | flops | bytes accessed | tf_op | source)
XLA Modules:
  0.0 46.7 jit_solution(11517358480197134867)
XLA Ops:
  0.0 45.8 %shard_map.64 = bf16[128,3072]{1,0:T(8,128)(2,1)S(1)} custom-call(bf16[128,3072]{1,0:T(8,128)(2,1)} %x_hbm.1, bf16[128,3072]{1,0:T(8,128)(2,1)} %dy_hbm.1, bf16[12,256,6,4,128]{4,3,2,1,0:T(4,128)(2,1)} %bitcast.4, bf16[4,256,3,2,4,128]{5,4,3,2,1,0:T(4,128)(2,1)} %bitcast.6, bf16[4,256,3,2,4,128]{5,4,3,2,1,0:T(4,128)(2,1)} %bitcast.7, ...), custom_call_target="tpu_custom_call" | custom-call | tf_op jit(solution)/shard_map/pallas_call | solution.py:445
  45.8 0.9 %copy.8 = bf16[128,3072]{1,0:T(8,128)(2,1)} copy(bf16[128,3072]{1,0:T(8,128)(2,1)S(1)} %shard_map.64) | data formatting | bytes 1572864

commit v4 on v1

--- a/solution.py
+++ b/solution.py
@@ -173,7 +173,6 @@
         do0_rows(q, (1, 2))
     for i in range(4):
         wkv_copy(wv_hbm, i, 4 + i).start()
-    swap_copy(0).start()
     with scope('relk'):
         for i in range(4):
             wait_slot(i)
@@ -182,6 +181,7 @@
         wo_copy(0, k).start()
     with scope('k_own'):
         k_rows(q)
+    swap_copy(0).start()
     with scope('xswap'):
         swap_copy(1).wait_recv()
     with scope('k_other'):

time: 46.8 us -> 46.8 us (level)
  no operation moved by 1% of the time
where the time goes in v4:
time: 46.8 us; the launch traced here: 46.7 us
  Pallas kernels  45.8 us (98%)
  local copies, waits for them, and re-layouts  0.88 us (2%)
    pallas_call x1, Pallas kernels, device_fn(): pl.pallas_call(kernel, out_shape=pltpu.VMEM((TOK, D), BF16), in_specs=[pl...  45.8 us

profile of v4, /device:TPU:0, one launch (start us, length us, event | category | flops | bytes accessed | tf_op | source)
XLA Modules:
  0.0 46.7 jit_solution(1134725450949334093)
XLA Ops:
  0.0 45.8 %shard_map.64 = bf16[128,3072]{1,0:T(8,128)(2,1)S(1)} custom-call(bf16[128,3072]{1,0:T(8,128)(2,1)} %x_hbm.1, bf16[128,3072]{1,0:T(8,128)(2,1)} %dy_hbm.1, bf16[12,256,6,4,128]{4,3,2,1,0:T(4,128)(2,1)} %bitcast.4, bf16[4,256,3,2,4,128]{5,4,3,2,1,0:T(4,128)(2,1)} %bitcast.6, bf16[4,256,3,2,4,128]{5,4,3,2,1,0:T(4,128)(2,1)} %bitcast.7, ...), custom_call_target="tpu_custom_call" | custom-call | tf_op jit(solution)/shard_map/pallas_call | solution.py:445
  45.8 0.9 %copy.8 = bf16[128,3072]{1,0:T(8,128)(2,1)} copy(bf16[128,3072]{1,0:T(8,128)(2,1)S(1)} %shard_map.64) | data formatting | bytes 1572864
